TPU v7x, 32 devices: a whole 2x2x4 slice. The times are simulated.
32 devices in a mesh: col: 8 (over y, x, core), grp: 4 (over z).
Axes of the slice: x: 2, y: 2, z: 4, core: 2. Of those that a mesh axis runs over, the one named last changes fastest.
Arguments:
- profiles: float32 [2048, 116], P('col'), may hold values from -6 to 6
- courant: float32 [2048, 58], P('col'), may hold values from -0.7 to 0.7
- owner_map: int32 [2048], replicated, may hold values from 0 to 2047, as said below
- cloud_flags: int32 [2048], P('col'), may hold values 0 or 1
- crm_state: float32 [2, 58, 64, 2048], P(None, None, 'grp', 'col'), may hold values from -6 to 6
Outputs:
- tendency: float32 [2048, 116], P('col')
- crm_final: float32 [2, 58, 64, 2048], P(None, None, 'grp', 'col')
Inputs may be any that keep to these rules, and one draw needn't show every extreme that they name: owner_map is a permutation; physics column p lives in span p // 256, element column e in group e // 256; each group hands at most 34 columns to one span, and exactly 34 to some spans, and every span receives exactly 256 columns.
All inputs are finite; a program needn't handle non-finite values. No bound on the sum of `cloud_flags` on one device may be relied on, other than what follows from the above.
Results may differ from a plain program's by a relative error of at most 0.00002.
Values sent between devices are 32-bit elements; how exact they have to be, the bound alone decides.
A program may use at most 64 MiB of HBM per device.

v0:
```python
import jax
import jax.numpy as jnp
from jax import lax
from jax.sharding import PartitionSpec as P

STEPS = 8
diffuse_x = 0.25
diffuse_z = 0.2
sat_scale = 0.5
sat_slope = 0.3
cond_rate = 0.5
latent_gain = 0.4


def padded(x, sides, width):
    for axis, dim in sides:
        peers, length = (lax.axis_size(axis), x.shape[dim])
        up = [(i, (i + 1) % peers) for i in range(peers)]
        down = [(j, i) for i, j in up]
        last = lax.slice_in_dim(x, length - width, length, axis=dim)
        leading = lax.slice_in_dim(x, 0, width, axis=dim)
        before = lax.ppermute(last, axis, up)
        after = lax.ppermute(leading, axis, down)
        x = jnp.concatenate([before, x, after], axis=dim)
    return x


def condense(fields, cloudy):
    energy = fields[0]
    moisture = fields[1]
    saturation = sat_scale * (jnp.exp(sat_slope * energy) - 1.0)
    amount = cond_rate * jnp.maximum(moisture - saturation, 0.0) * cloudy
    return jnp.stack([energy + latent_gain * amount, moisture - amount])


def advance(widened, courant_here, forcing, cloudy):
    centre = widened[:, :, 1:-1]
    eastern = widened[:, :, 2:]
    western = widened[:, :, :-2]
    upper = jnp.concatenate([centre[:, 1:], centre[:, -1:]], axis=1)
    lower = jnp.concatenate([centre[:, :1], centre[:, :-1]], axis=1)
    stepped = (
        centre
        + courant_here * ((western - eastern) * 0.5)
        + diffuse_x * (eastern - 2.0 * centre + western)
        + diffuse_z * (upper - 2.0 * centre + lower)
        + forcing
    )
    return condense(stepped, cloudy)


def on_device(profiles, courant, owner_map, cloud_flags, crm_state):
    columns = profiles.shape[0]
    levels = courant.shape[1]
    col_count = lax.axis_size("col")
    col_index = lax.axis_index("col")
    per_peer = columns // col_count
    capacity = per_peer + min(2, per_peer)
    positions = jnp.arange(columns, dtype=jnp.int32)
    my_owner = lax.dynamic_slice_in_dim(owner_map, col_index * columns, columns)
    target = my_owner // columns
    earlier = (target[:, None] == target[None, :]) & (positions[None, :] < positions[:, None])
    order_in = jnp.sum(earlier.astype(jnp.int32), axis=1)
    sent_slot = target * capacity + order_in
    send_rows = jnp.full((col_count * capacity,), columns, jnp.int32).at[sent_slot].set(positions)
    padded_prof = jnp.concatenate([profiles, jnp.zeros((1, profiles.shape[1]), jnp.float32)])
    padded_cour = jnp.concatenate([courant, jnp.zeros((1, levels), jnp.float32)])
    out_prof = padded_prof[send_rows].reshape(col_count, capacity, profiles.shape[1])
    out_cour = padded_cour[send_rows].reshape(col_count, capacity, levels)
    got_prof, got_cour = (
        lax.all_to_all(out_prof, "col", split_axis=0, concat_axis=0, tiled=True),
        lax.all_to_all(out_cour, "col", split_axis=0, concat_axis=0, tiled=True),
    )
    block_view = owner_map.reshape(col_count, columns)
    landing = (block_view // columns == col_index).astype(jnp.int32)
    before = jnp.cumsum(landing, axis=1) - landing
    sources = jnp.arange(col_count, dtype=jnp.int32)[:, None]
    where_from = sources * capacity + before
    landing_slot = jnp.where(landing > 0, block_view - col_index * columns, columns)
    senders_block = 4
    slot_blocks = landing_slot.reshape(col_count // senders_block, senders_block * columns)
    from_blocks = where_from.reshape(col_count // senders_block, senders_block * columns)

    def match_block(found, pair):
        slots, anchors = pair
        hits = slots[None, :] == positions[:, None]
        return (found + jnp.sum(jnp.where(hits, anchors[None, :], 0), axis=1), None)

    take_rows, unused = lax.scan(
        match_block, jnp.zeros((columns,), jnp.int32), (slot_blocks, from_blocks)
    )
    phys_prof = got_prof.reshape(col_count * capacity, profiles.shape[1])[take_rows]
    phys_cour = got_cour.reshape(col_count * capacity, levels)[take_rows]
    forcing = (phys_prof.reshape(columns, 2, levels).transpose(1, 2, 0) / STEPS)[:, :, None, :]
    courant_here = phys_cour.T[None, :, None, :]
    cloudy = cloud_flags.astype(jnp.float32)
    crm_now = crm_state
    for repeat in range(STEPS // 2):
        widened = padded(crm_now, (("grp", 2),), 2)
        middle = advance(widened, courant_here, forcing, cloudy)
        crm_now = advance(middle, courant_here, forcing, cloudy)
    cells_all = crm_state.shape[2] * lax.axis_size("grp")
    partial_value = jnp.sum(crm_now, axis=2) - jnp.sum(crm_state, axis=2)
    totals = lax.psum(partial_value, "grp")
    increment = totals / cells_all
    phys_inc = increment.transpose(2, 0, 1).reshape(columns, 2 * levels)
    back_rows = (
        jnp.zeros((col_count * capacity, 2 * levels), jnp.float32).at[take_rows].set(phys_inc)
    )
    got_back = lax.all_to_all(
        back_rows.reshape(col_count, capacity, 2 * levels),
        "col",
        split_axis=0,
        concat_axis=0,
        tiled=True,
    )
    tendency = got_back.reshape(col_count * capacity, 2 * levels)[sent_slot]
    return (tendency, crm_now)


def solution(mesh):
    placed = (P("col", None), P("col", None), P(), P("col"), P(None, None, "grp", "col"))
    return jax.shard_map(
        on_device,
        mesh=mesh,
        in_specs=placed,
        out_specs=(P("col", None), P(None, None, "grp", "col")),
        check_vma=False,
    )
```

profile of v0, /device:TPU:0, one launch (start us, length us, event | category | flops | bytes accessed | tf_op | source)
XLA Modules:
  0.0 158.9 jit_solution(1841023109057067718)
XLA Ops:
  7.2 0.9 and_select_fusion.1
  8.3 0.8 compare_select_fusion.2
  9.1 1.4 scatter_custom_fusion
  10.5 0.9 copy.71
  11.5 1.1 gather_fusion
  12.6 0.9 reshape.148
  13.4 5.2 %all-to-all-start = ((f32[8,1,1972]{2,1,0:T(1,128)}), f32[8,1,1972]{2,1,0:T(1,128)S(1)}, u32[]{:S(2)}, u32[]{:S(2)}) async-start(f32[8,1,1972]{2,1,0:T(1,128)} %reshape.148), calls=%async_computation | async-start | bytes 131072 | tf_op jit(solution)/shard_map/all_to_all | solution.py:72
  18.8 1.6 %collective-permute-start = (f32[2,58,2,256]{3,1,2,0:T(8,128)S(1)}, f32[2,58,2,256]{3,1,2,0:T(8,128)S(1)}, u32[]{:S(2)}, u32[]{:S(2)}) collective-permute-start(f32[2,58,2,256]{3,1,2,0:T(8,128)S(1)} %copy.84), channel_id=1, source_target_pairs={{0,1},{1,2},{2,3},{3,0},{4,5},{5,6},{6,7},{7,4},{8,9},{9,10},{10,1... | collective-permute-start | bytes 712712 | tf_op jit(solution)/shard_map/ppermute | solution.py:22
  20.5 2.3 %collective-permute-start.1 = (f32[2,58,2,256]{3,1,2,0:T(8,128)S(1)}, f32[2,58,2,256]{3,1,2,0:T(8,128)S(1)}, u32[]{:S(2)}, u32[]{:S(2)}) collective-permute-start(f32[2,58,2,256]{3,1,2,0:T(8,128)S(1)} %copy.85), channel_id=1, source_target_pairs={{1,0},{2,1},{3,2},{0,3},{5,4},{6,5},{7,6},{4,7},{9,8},{10,9},{11,1... | collective-permute-start | bytes 712712 | tf_op jit(solution)/shard_map/ppermute | solution.py:23
  24.6 1.1 gather_fusion.2
  25.6 0.7 reshape.75
  26.3 4.2 %all-to-all-start.1 = ((f32[8,34,116]{2,1,0:T(8,128)}), f32[8,34,116]{2,1,0:T(8,128)S(1)}, u32[]{:S(2)}, u32[]{:S(2)}) async-start(f32[8,34,116]{2,1,0:T(8,128)} %reshape.75), calls=%async_computation.1 | async-start | bytes 327680 | tf_op jit(solution)/shard_map/all_to_all | solution.py:71
  31.1 0.8 reduce.2
  32.0 0.7 gather_fusion.1
  32.9 3.5 %all-to-all-done.1 = f32[8,34,116]{2,1,0:T(8,128)S(1)} async-done(((f32[8,34,116]{2,1,0:T(8,128)}), f32[8,34,116]{2,1,0:T(8,128)S(1)}, u32[]{:S(2)}, u32[]{:S(2)}) %all-to-all-start.1) | async-done | bytes 126240 | tf_op jit(solution)/shard_map/all_to_all | solution.py:71
  36.4 0.7 gather_fusion.3
  37.3 1.3 constant_dynamic-update-slice_fusion.6
  39.4 1.8 %fusion.44 = f32[2,58,18,256]{3,1,2,0:T(8,128)S(1)} fusion(f32[2,1,18,256]{3,1,2,0:T(1,128)S(1)} %get-tuple-element.78, f32[2,57,18,256]{3,1,2,0:T(8,128)S(1)} %get-tuple-element.80, f32[2,57,18,256]{3,1,2,0:T(8,128)S(1)} %get-tuple-element.79, f32[2,1,18,256]{3,1,2,0:T(1,128)S(1)} %get-tuple-element.77, f32[2,58,18,256]{3,1,2,0:T(8,128)S(1)} %get-tuple-element.115, ...), kind=kLoop, calls=%fused_computation.133 | loop fusion | flops 8017920 | bytes 13006848 | tf_op jit(solution)/shard_map/add | solution.py:43
  42.0 1.7 %fusion.80 = f32[2,58,16,256]{3,1,2,0:T(8,128)S(1)} fusion(f32[1,58,18,256]{3,1,2,0:T(8,128)S(1)} %get-tuple-element.88, f32[1,58,18,256]{3,1,2,0:T(8,128)S(1)} %get-tuple-element.87, f32[2,1,16,256]{3,1,2,0:T(1,128)S(1)} %get-tuple-element.96, f32[2,57,16,256]{3,1,2,0:T(8,128)S(1)} %fusion.60, f32[2,1,16,256]{3,1,2,0:T(1,128)S(1)} %get-tuple-element.95, ...), kind=kLoop, calls=%fused_computation.179 | loop fusion | flops 9027584 | bytes 6150144 | tf_op jit(solution)/shard_map/add | solution.py:43
  44.3 3.8 %collective-permute-start.3 = (f32[2,58,2,256]{3,1,2,0:T(8,128)S(1)}, f32[2,58,2,256]{3,1,2,0:T(8,128)S(1)}, u32[]{:S(2)}, u32[]{:S(2)}) collective-permute-start(f32[2,58,2,256]{3,1,2,0:T(8,128)S(1)} %get-tuple-element.111), channel_id=1, source_target_pairs={{1,0},{2,1},{3,2},{0,3},{5,4},{6,5},{7,6},{4,7},{9,8},{10,9},{11,1... | collective-permute-start | bytes 712712 | tf_op jit(solution)/shard_map/ppermute | solution.py:23
  48.1 7.2 %collective-permute-done.2 = f32[2,58,2,256]{3,1,2,0:T(8,128)S(1)} collective-permute-done((f32[2,58,2,256]{3,1,2,0:T(8,128)S(1)}, f32[2,58,2,256]{3,1,2,0:T(8,128)S(1)}, u32[]{:S(2)}, u32[]{:S(2)}) %collective-permute-start.2) | collective-permute-done | bytes 237600 | tf_op jit(solution)/shard_map/ppermute | solution.py:22
  55.2 2.6 %collective-permute-done.3 = f32[2,58,2,256]{3,1,2,0:T(8,128)S(1)} collective-permute-done((f32[2,58,2,256]{3,1,2,0:T(8,128)S(1)}, f32[2,58,2,256]{3,1,2,0:T(8,128)S(1)}, u32[]{:S(2)}, u32[]{:S(2)}) %collective-permute-start.3) | collective-permute-done | bytes 237600 | tf_op jit(solution)/shard_map/ppermute | solution.py:23
  58.1 0.6 fusion.109
  58.8 2.2 %fusion.10 = f32[2,58,18,256]{3,1,2,0:T(8,128)S(1)} fusion(f32[1,58,16,256]{3,1,2,0:T(8,128)S(1)} %get-tuple-element.104, f32[1,58,16,256]{3,1,2,0:T(8,128)S(1)} %get-tuple-element.103, f32[2,58,2,256]{3,1,2,0:T(8,128)S(1)} %collective-permute-done.2, f32[2,58,2,256]{3,1,2,0:T(8,128)S(1)} %collective-permute-done.3, ...), kind=kLoop, calls=%fused_computation.96 | loop fusion | flops 18708480 | bytes 11032576 | tf_op jit(solution)/shard_map/add | solution.py:43
  61.7 1.7 %fusion.75 = f32[2,58,16,256]{3,1,2,0:T(8,128)S(1)} fusion(f32[1,58,18,256]{3,1,2,0:T(8,128)S(1)} %get-tuple-element.86, f32[1,58,18,256]{3,1,2,0:T(8,128)S(1)} %get-tuple-element.85, f32[2,1,16,256]{3,1,2,0:T(1,128)S(1)} %get-tuple-element.94, f32[2,57,16,256]{3,1,2,0:T(8,128)S(1)} %fusion.56, f32[2,1,16,256]{3,1,2,0:T(1,128)S(1)} %get-tuple-element.93, ...), kind=kLoop, calls=%fused_computation.173 | loop fusion | flops 9027584 | bytes 6150144 | tf_op jit(solution)/shard_map/add | solution.py:43
  63.9 0.9 collective-permute-start.4
  64.8 3.0 %collective-permute-start.5 = (f32[2,58,2,256]{3,1,2,0:T(8,128)S(1)}, f32[2,58,2,256]{3,1,2,0:T(8,128)S(1)}, u32[]{:S(2)}, u32[]{:S(2)}) collective-permute-start(f32[2,58,2,256]{3,1,2,0:T(8,128)S(1)} %get-tuple-element.109), channel_id=1, source_target_pairs={{1,0},{2,1},{3,2},{0,3},{5,4},{6,5},{7,6},{4,7},{9,8},{10,9},{11,1... | collective-permute-start | bytes 712712 | tf_op jit(solution)/shard_map/ppermute | solution.py:23
  67.8 7.2 %collective-permute-done.4 = f32[2,58,2,256]{3,1,2,0:T(8,128)S(1)} collective-permute-done((f32[2,58,2,256]{3,1,2,0:T(8,128)S(1)}, f32[2,58,2,256]{3,1,2,0:T(8,128)S(1)}, u32[]{:S(2)}, u32[]{:S(2)}) %collective-permute-start.4) | collective-permute-done | bytes 237600 | tf_op jit(solution)/shard_map/ppermute | solution.py:22
  75.0 2.3 %collective-permute-done.5 = f32[2,58,2,256]{3,1,2,0:T(8,128)S(1)} collective-permute-done((f32[2,58,2,256]{3,1,2,0:T(8,128)S(1)}, f32[2,58,2,256]{3,1,2,0:T(8,128)S(1)}, u32[]{:S(2)}, u32[]{:S(2)}) %collective-permute-start.5) | collective-permute-done | bytes 237600 | tf_op jit(solution)/shard_map/ppermute | solution.py:23
  78.2 2.2 %fusion.23 = f32[2,58,18,256]{3,1,2,0:T(8,128)S(1)} fusion(f32[1,58,16,256]{3,1,2,0:T(8,128)S(1)} %get-tuple-element.102, f32[1,58,16,256]{3,1,2,0:T(8,128)S(1)} %get-tuple-element.101, f32[2,58,2,256]{3,1,2,0:T(8,128)S(1)} %collective-permute-done.4, f32[2,58,2,256]{3,1,2,0:T(8,128)S(1)} %collective-permute-done.5, ...), kind=kLoop, calls=%fused_computation.109 | loop fusion | flops 18708480 | bytes 11032576 | tf_op jit(solution)/shard_map/add | solution.py:43
  81.1 1.7 %fusion.70 = f32[2,58,16,256]{3,1,2,0:T(8,128)S(1)} fusion(f32[1,58,18,256]{3,1,2,0:T(8,128)S(1)} %get-tuple-element.84, f32[1,58,18,256]{3,1,2,0:T(8,128)S(1)} %get-tuple-element.83, f32[2,1,16,256]{3,1,2,0:T(1,128)S(1)} %get-tuple-element.92, f32[2,57,16,256]{3,1,2,0:T(8,128)S(1)} %fusion.52, f32[2,1,16,256]{3,1,2,0:T(1,128)S(1)} %get-tuple-element.91, ...), kind=kLoop, calls=%fused_computation.167 | loop fusion | flops 9027584 | bytes 6150144 | tf_op jit(solution)/shard_map/add | solution.py:43
  83.2 1.7 %collective-permute-start.6 = (f32[2,58,2,256]{3,1,2,0:T(8,128)S(1)}, f32[2,58,2,256]{3,1,2,0:T(8,128)S(1)}, u32[]{:S(2)}, u32[]{:S(2)}) collective-permute-start(f32[2,58,2,256]{3,1,2,0:T(8,128)S(1)} %get-tuple-element.108), channel_id=1, source_target_pairs={{0,1},{1,2},{2,3},{3,0},{4,5},{5,6},{6,7},{7,4},{8,9},{9,10},{10,1... | collective-permute-start | bytes 712712 | tf_op jit(solution)/shard_map/ppermute | solution.py:22
  84.9 2.2 %collective-permute-start.7 = (f32[2,58,2,256]{3,1,2,0:T(8,128)S(1)}, f32[2,58,2,256]{3,1,2,0:T(8,128)S(1)}, u32[]{:S(2)}, u32[]{:S(2)}) collective-permute-start(f32[2,58,2,256]{3,1,2,0:T(8,128)S(1)} %get-tuple-element.107), channel_id=1, source_target_pairs={{1,0},{2,1},{3,2},{0,3},{5,4},{6,5},{7,6},{4,7},{9,8},{10,9},{11,1... | collective-permute-start | bytes 712712 | tf_op jit(solution)/shard_map/ppermute | solution.py:23
  87.1 1.9 %reduce_sum.38 = f32[2,58,256]{2,1,0:T(8,128)S(1)} reduce(f32[2,58,16,256]{3,2,1,0:T(8,128)} %param.11, f32[]{:T(128)} %constant.35.clone.1), dimensions={2}, to_apply=%region_8.9 | reduce | flops 445440 | bytes 2019332 | tf_op jit(solution)/shard_map/reduce_sum | solution.py:103
  89.0 5.3 %collective-permute-done.6 = f32[2,58,2,256]{3,1,2,0:T(8,128)S(1)} collective-permute-done((f32[2,58,2,256]{3,1,2,0:T(8,128)S(1)}, f32[2,58,2,256]{3,1,2,0:T(8,128)S(1)}, u32[]{:S(2)}, u32[]{:S(2)}) %collective-permute-start.6) | collective-permute-done | bytes 237600 | tf_op jit(solution)/shard_map/ppermute | solution.py:22
  94.3 3.6 %collective-permute-done.7 = f32[2,58,2,256]{3,1,2,0:T(8,128)S(1)} collective-permute-done((f32[2,58,2,256]{3,1,2,0:T(8,128)S(1)}, f32[2,58,2,256]{3,1,2,0:T(8,128)S(1)}, u32[]{:S(2)}, u32[]{:S(2)}) %collective-permute-start.7) | collective-permute-done | bytes 237600 | tf_op jit(solution)/shard_map/ppermute | solution.py:23
  98.7 2.0 %fusion.36 = f32[2,58,18,256]{3,1,2,0:T(8,128)S(1)} fusion(f32[1,58,16,256]{3,1,2,0:T(8,128)S(1)} %get-tuple-element.100, f32[1,58,16,256]{3,1,2,0:T(8,128)S(1)} %get-tuple-element.99, f32[2,58,2,256]{3,1,2,0:T(8,128)S(1)} %collective-permute-done.6, f32[2,58,2,256]{3,1,2,0:T(8,128)S(1)} %collective-permute-done.7, ...), kind=kLoop, calls=%fused_computation.122 | loop fusion | flops 18708480 | bytes 11032576 | tf_op jit(solution)/shard_map/add | solution.py:43
  101.5 1.7 %fusion.65 = f32[2,58,16,256]{3,1,2,0:T(8,128)S(1)} fusion(f32[1,58,18,256]{3,1,2,0:T(8,128)S(1)} %get-tuple-element.82, f32[1,58,18,256]{3,1,2,0:T(8,128)S(1)} %get-tuple-element.81, f32[2,1,16,256]{3,1,2,0:T(1,128)S(1)} %get-tuple-element.90, f32[2,57,16,256]{3,1,2,0:T(8,128)S(1)} %fusion.48, f32[2,1,16,256]{3,1,2,0:T(1,128)S(1)} %get-tuple-element.89, ...), kind=kLoop, calls=%fused_computation.161 | loop fusion | flops 9027584 | bytes 6150144 | tf_op jit(solution)/shard_map/add | solution.py:43
  103.8 0.7 sub.250
  104.5 33.6 %all-reduce.4.cloned.1.call-done = f32[2,58,256]{2,1,0:T(8,128)} async-done(((f32[2,58,256]{2,1,0:T(8,128)}), f32[2,58,256]{2,1,0:T(8,128)}) %all-reduce.4.cloned.1.call-update) | async-done | bytes 118800 | tf_op jit(solution)/shard_map/psum | solution.py:104
  138.1 0.9 multiply_bitcast_fusion
  139.2 1.2 scatter_custom_fusion.1
  140.3 0.7 reshape.78
  141.0 3.6 %all-to-all-start.2 = ((f32[8,34,116]{2,1,0:T(8,128)}), f32[8,34,116]{2,1,0:T(8,128)S(1)}, u32[]{:S(2)}, u32[]{:S(2)}) async-start(f32[8,34,116]{2,1,0:T(8,128)} %reshape.78), calls=%async_computation.2 | async-start | bytes 327680 | tf_op jit(solution)/shard_map/all_to_all | solution.py:110
  144.7 2.4 %copy.78 = f32[2,58,16,256]{3,2,1,0:T(8,128)} copy(f32[2,58,16,256]{3,1,2,0:T(8,128)S(1)} %get-tuple-element.105) | data formatting | bytes 3801088
  147.0 3.5 %all-to-all-done.2 = f32[8,34,116]{2,1,0:T(8,128)S(1)} async-done(((f32[8,34,116]{2,1,0:T(8,128)}), f32[8,34,116]{2,1,0:T(8,128)S(1)}, u32[]{:S(2)}, u32[]{:S(2)}) %all-to-all-start.2) | async-done | bytes 126240 | tf_op jit(solution)/shard_map/all_to_all | solution.py:110
  150.5 0.7 gather_fusion.4
  151.3 0.8 copy.77
  (92 shorter events, 11.5 us)
Async XLA Ops:
  7.2 15.6 %copy-start.2 = (s32[2048]{0:T(1024)S(1)}, s32[2048]{0:T(1024)}, u32[]{:S(2)}) copy-start(s32[2048]{0:T(1024)} %param.9) | copy-start | bytes 24580
  7.2 11.4 %copy-start = (f32[2,58,16,256]{3,2,1,0:T(8,128)S(1)}, f32[2,58,16,256]{3,2,1,0:T(8,128)}, u32[]{:S(2)}) copy-start(f32[2,58,16,256]{3,2,1,0:T(8,128)} %param.11) | copy-start | bytes 5701636
  11.4 13.0 %copy-start.3 = (s32[256]{0:T(256)S(1)}, s32[256]{0:T(256)}, u32[]{:S(2)}) copy-start(s32[256]{0:T(256)} %param.10) | copy-start | bytes 3076
  11.4 13.0 %copy-start.1 = (f32[256,116]{0,1:T(8,128)S(1)}, f32[256,116]{0,1:T(8,128)}, u32[]{:S(2)}) copy-start(f32[256,116]{0,1:T(8,128)} %param.7) | copy-start | bytes 356356
  13.4 12.9 %all-to-all-start = ((f32[8,1,1972]{2,1,0:T(1,128)}), f32[8,1,1972]{2,1,0:T(1,128)S(1)}, u32[]{:S(2)}, u32[]{:S(2)}) async-start(f32[8,1,1972]{2,1,0:T(1,128)} %reshape.148), calls=%async_computation | async-start | bytes 131072 | tf_op jit(solution)/shard_map/all_to_all | solution.py:72
  18.8 18.4 %collective-permute-start = (f32[2,58,2,256]{3,1,2,0:T(8,128)S(1)}, f32[2,58,2,256]{3,1,2,0:T(8,128)S(1)}, u32[]{:S(2)}, u32[]{:S(2)}) collective-permute-start(f32[2,58,2,256]{3,1,2,0:T(8,128)S(1)} %copy.84), channel_id=1, source_target_pairs={{0,1},{1,2},{2,3},{3,0},{4,5},{5,6},{6,7},{7,4},{8,9},{9,10},{10,1... | collective-permute-start | bytes 712712 | tf_op jit(solution)/shard_map/ppermute | solution.py:22
  20.5 18.2 %collective-permute-start.1 = (f32[2,58,2,256]{3,1,2,0:T(8,128)S(1)}, f32[2,58,2,256]{3,1,2,0:T(8,128)S(1)}, u32[]{:S(2)}, u32[]{:S(2)}) collective-permute-start(f32[2,58,2,256]{3,1,2,0:T(8,128)S(1)} %copy.85), channel_id=1, source_target_pairs={{1,0},{2,1},{3,2},{0,3},{5,4},{6,5},{7,6},{4,7},{9,8},{10,9},{11,1... | collective-permute-start | bytes 712712 | tf_op jit(solution)/shard_map/ppermute | solution.py:23
  26.3 10.0 %all-to-all-start.1 = ((f32[8,34,116]{2,1,0:T(8,128)}), f32[8,34,116]{2,1,0:T(8,128)S(1)}, u32[]{:S(2)}, u32[]{:S(2)}) async-start(f32[8,34,116]{2,1,0:T(8,128)} %reshape.75), calls=%async_computation.1 | async-start | bytes 327680 | tf_op jit(solution)/shard_map/all_to_all | solution.py:71
  30.5 107.6 %all-reduce.4.cloned.1.call-start = ((), (), s32[]{:S(2)}) async-start(), calls=%async_computation.3 | async-start | bytes 262144 | tf_op jit(solution)/shard_map/psum | solution.py:104
  44.2 11.0 %collective-permute-start.2 = (f32[2,58,2,256]{3,1,2,0:T(8,128)S(1)}, f32[2,58,2,256]{3,1,2,0:T(8,128)S(1)}, u32[]{:S(2)}, u32[]{:S(2)}) collective-permute-start(f32[2,58,2,256]{3,1,2,0:T(8,128)S(1)} %get-tuple-element.112), channel_id=1, source_target_pairs={{0,1},{1,2},{2,3},{3,0},{4,5},{5,6},{6,7},{7,4},{8,9},{9,10},{10,1... | collective-permute-start | bytes 712712 | tf_op jit(solution)/shard_map/ppermute | solution.py:22
  44.3 13.6 %collective-permute-start.3 = (f32[2,58,2,256]{3,1,2,0:T(8,128)S(1)}, f32[2,58,2,256]{3,1,2,0:T(8,128)S(1)}, u32[]{:S(2)}, u32[]{:S(2)}) collective-permute-start(f32[2,58,2,256]{3,1,2,0:T(8,128)S(1)} %get-tuple-element.111), channel_id=1, source_target_pairs={{1,0},{2,1},{3,2},{0,3},{5,4},{6,5},{7,6},{4,7},{9,8},{10,9},{11,1... | collective-permute-start | bytes 712712 | tf_op jit(solution)/shard_map/ppermute | solution.py:23
  63.9 11.0 %collective-permute-start.4 = (f32[2,58,2,256]{3,1,2,0:T(8,128)S(1)}, f32[2,58,2,256]{3,1,2,0:T(8,128)S(1)}, u32[]{:S(2)}, u32[]{:S(2)}) collective-permute-start(f32[2,58,2,256]{3,1,2,0:T(8,128)S(1)} %get-tuple-element.110), channel_id=1, source_target_pairs={{0,1},{1,2},{2,3},{3,0},{4,5},{5,6},{6,7},{7,4},{8,9},{9,10},{10,1... | collective-permute-start | bytes 712712 | tf_op jit(solution)/shard_map/ppermute | solution.py:22
  64.8 12.4 %collective-permute-start.5 = (f32[2,58,2,256]{3,1,2,0:T(8,128)S(1)}, f32[2,58,2,256]{3,1,2,0:T(8,128)S(1)}, u32[]{:S(2)}, u32[]{:S(2)}) collective-permute-start(f32[2,58,2,256]{3,1,2,0:T(8,128)S(1)} %get-tuple-element.109), channel_id=1, source_target_pairs={{1,0},{2,1},{3,2},{0,3},{5,4},{6,5},{7,6},{4,7},{9,8},{10,9},{11,1... | collective-permute-start | bytes 712712 | tf_op jit(solution)/shard_map/ppermute | solution.py:23
  83.2 11.1 %collective-permute-start.6 = (f32[2,58,2,256]{3,1,2,0:T(8,128)S(1)}, f32[2,58,2,256]{3,1,2,0:T(8,128)S(1)}, u32[]{:S(2)}, u32[]{:S(2)}) collective-permute-start(f32[2,58,2,256]{3,1,2,0:T(8,128)S(1)} %get-tuple-element.108), channel_id=1, source_target_pairs={{0,1},{1,2},{2,3},{3,0},{4,5},{5,6},{6,7},{7,4},{8,9},{9,10},{10,1... | collective-permute-start | bytes 712712 | tf_op jit(solution)/shard_map/ppermute | solution.py:22
  84.9 13.0 %collective-permute-start.7 = (f32[2,58,2,256]{3,1,2,0:T(8,128)S(1)}, f32[2,58,2,256]{3,1,2,0:T(8,128)S(1)}, u32[]{:S(2)}, u32[]{:S(2)}) collective-permute-start(f32[2,58,2,256]{3,1,2,0:T(8,128)S(1)} %get-tuple-element.107), channel_id=1, source_target_pairs={{1,0},{2,1},{3,2},{0,3},{5,4},{6,5},{7,6},{4,7},{9,8},{10,9},{11,1... | collective-permute-start | bytes 712712 | tf_op jit(solution)/shard_map/ppermute | solution.py:23
  141.0 9.5 %all-to-all-start.2 = ((f32[8,34,116]{2,1,0:T(8,128)}), f32[8,34,116]{2,1,0:T(8,128)S(1)}, u32[]{:S(2)}, u32[]{:S(2)}) async-start(f32[8,34,116]{2,1,0:T(8,128)} %reshape.78), calls=%async_computation.2 | async-start | bytes 327680 | tf_op jit(solution)/shard_map/all_to_all | solution.py:110
Sparse Core Ops, SparseCore 0:
  104.6 33.4 all-reduce.3
where the time goes:
time: 159 us
  waiting for transfers between devices  68.8 us (43%)
  starting transfers between devices  28.6 us (18%)
  other arithmetic  28 us (18%)
  local copies, waits for them, and re-layouts  18.8 us (12%)
  between operations  14.7 us (9%)
    psum x1, waiting for transfers between devices, on_device(): totals = lax.psum(partial_value, 'grp')  33.6 us
    ppermute x4, waiting for transfers between devices, padded(): before = lax.ppermute(last, axis, up)  19.6 us
    add x8, other arithmetic, advance(): centre + courant_here * ((western - eastern) * 0.5)  14.8 us
    ppermute x4, starting transfers between devices, padded(): after = lax.ppermute(leading, axis, down)  11.3 us
    ppermute x4, waiting for transfers between devices, padded(): after = lax.ppermute(leading, axis, down)  8.52 us
    unnamed x20, local copies, waits for them, and re-layouts  6.61 us
    all_to_all x1, starting transfers between devices, on_device(): lax.all_to_all(out_cour, 'col', split_axis=0, concat_axis=0, tiled=True)  5.2 us
    ppermute x4, starting transfers between devices, padded(): before = lax.ppermute(last, axis, up)  4.24 us
  transfers between devices with their start and end apart: 12, of which 9 were waited for; matrix products, arithmetic and copies ran while one was open for 8% of the time, Pallas kernels for 0%

commit v1 on v0

--- a/solution.py
+++ b/solution.py
@@ -10,6 +10,12 @@
 sat_slope = 0.3
 cond_rate = 0.5
 latent_gain = 0.4
+
+
+def add_all(x, axis):
+    pieces = lax.all_gather(x, axis, axis=0, tiled=False)
+    result = pieces.sum(axis=0)
+    return result
 
 
 def padded(x, sides, width):
@@ -101,7 +107,7 @@
         crm_now = advance(middle, courant_here, forcing, cloudy)
     cells_all = crm_state.shape[2] * lax.axis_size("grp")
     partial_value = jnp.sum(crm_now, axis=2) - jnp.sum(crm_state, axis=2)
-    totals = lax.psum(partial_value, "grp")
+    totals = add_all(partial_value, "grp")
     increment = totals / cells_all
     phys_inc = increment.transpose(2, 0, 1).reshape(columns, 2 * levels)
     back_rows = (

time: 159 us -> 126 us (0.79)
  waiting for transfers between devices: 68.8 us -> 35.1 us
  blocking collectives: 0 us -> 15.9 us
  between operations: 14.7 us -> 1.3 us
  other arithmetic: 28 us -> 26.4 us
    psum x1 -> x0, waiting for transfers between devices: 33.6 us -> none  [on_device(): totals = lax.psum(partial_value, 'grp')]
    all_gather x0 -> x1, blocking collectives: none -> 15.9 us  [add_all(): pieces = lax.all_gather(x, axis, axis=0, tiled=False)]
  transfers between devices with their start and end apart: 12 -> 11, of which waited for: 9 -> 8; matrix products, arithmetic and copies ran while one was open for 8% -> 10% of each run, Pallas kernels for 0% -> 0%
where the time goes in v1:
time: 126 us
  waiting for transfers between devices  35.1 us (28%)
  starting transfers between devices  28.3 us (22%)
  other arithmetic  26.4 us (21%)
  local copies, waits for them, and re-layouts  18.8 us (15%)
  blocking collectives  15.9 us (13%)
  between operations  1.3 us (1%)
    ppermute x4, waiting for transfers between devices, padded(): before = lax.ppermute(last, axis, up)  19.6 us
    all_gather x1, blocking collectives, add_all(): pieces = lax.all_gather(x, axis, axis=0, tiled=False)  15.9 us
    add x8, other arithmetic, advance(): centre + courant_here * ((western - eastern) * 0.5)  14.8 us
    ppermute x4, starting transfers between devices, padded(): after = lax.ppermute(leading, axis, down)  11.3 us
    ppermute x4, waiting for transfers between devices, padded(): after = lax.ppermute(leading, axis, down)  8.52 us
    unnamed x20, local copies, waits for them, and re-layouts  6.61 us
    all_to_all x1, starting transfers between devices, on_device(): lax.all_to_all(out_cour, 'col', split_axis=0, concat_axis=0, tiled=True)  5.2 us
    ppermute x4, starting transfers between devices, padded(): before = lax.ppermute(last, axis, up)  4.24 us
  transfers between devices with their start and end apart: 11, of which 8 were waited for; matrix products, arithmetic and copies ran while one was open for 10% of the time, Pallas kernels for 0%

profile of v1, /device:TPU:0, one launch (start us, length us, event | category | flops | bytes accessed | tf_op | source)
XLA Modules:
  0.0 125.9 jit_solution(2607312403916868964)
XLA Ops:
  0.7 0.9 and_select_fusion.1
  1.7 0.8 compare_select_fusion.2
  2.5 1.4 %scatter_custom_fusion = s32[272]{0:T(512)S(1)} fusion(s32[256]{0:T(256)S(1)} %compare_select_fusion.2, s32[256]{0:T(256)S(1)} %iota.32, s32[]{:T(128)} %constant.48.clone.1), kind=kCustom, calls=%fused_computation.268 | custom fusion | bytes 1092 | tf_op jit(solution)/shard_map/scatter | solution.py:71
  4.0 0.9 copy.71
  4.9 1.1 gather_fusion
  6.0 0.9 reshape.161
  6.9 5.2 %all-to-all-start = ((f32[8,1,1972]{2,1,0:T(1,128)}), f32[8,1,1972]{2,1,0:T(1,128)S(1)}, u32[]{:S(2)}, u32[]{:S(2)}) async-start(f32[8,1,1972]{2,1,0:T(1,128)} %reshape.161), calls=%async_computation | async-start | bytes 131072 | tf_op jit(solution)/shard_map/all_to_all | solution.py:78
  12.3 1.6 %collective-permute-start = (f32[2,58,2,256]{3,1,2,0:T(8,128)S(1)}, f32[2,58,2,256]{3,1,2,0:T(8,128)S(1)}, u32[]{:S(2)}, u32[]{:S(2)}) collective-permute-start(f32[2,58,2,256]{3,1,2,0:T(8,128)S(1)} %copy.84), channel_id=1, source_target_pairs={{0,1},{1,2},{2,3},{3,0},{4,5},{5,6},{6,7},{7,4},{8,9},{9,10},{10,1... | collective-permute-start | bytes 712712 | tf_op jit(solution)/shard_map/ppermute | solution.py:28
  13.9 2.3 %collective-permute-start.1 = (f32[2,58,2,256]{3,1,2,0:T(8,128)S(1)}, f32[2,58,2,256]{3,1,2,0:T(8,128)S(1)}, u32[]{:S(2)}, u32[]{:S(2)}) collective-permute-start(f32[2,58,2,256]{3,1,2,0:T(8,128)S(1)} %copy.85), channel_id=1, source_target_pairs={{1,0},{2,1},{3,2},{0,3},{5,4},{6,5},{7,6},{4,7},{9,8},{10,9},{11,1... | collective-permute-start | bytes 712712 | tf_op jit(solution)/shard_map/ppermute | solution.py:29
  18.1 1.1 gather_fusion.2
  19.1 0.7 reshape.87
  19.8 4.2 %all-to-all-start.1 = ((f32[8,34,116]{2,1,0:T(8,128)}), f32[8,34,116]{2,1,0:T(8,128)S(1)}, u32[]{:S(2)}, u32[]{:S(2)}) async-start(f32[8,34,116]{2,1,0:T(8,128)} %reshape.87), calls=%async_computation.1 | async-start | bytes 327680 | tf_op jit(solution)/shard_map/all_to_all | solution.py:77
  24.5 0.8 reduce.2
  25.4 0.7 gather_fusion.1
  26.3 3.6 %all-to-all-done.1 = f32[8,34,116]{2,1,0:T(8,128)S(1)} async-done(((f32[8,34,116]{2,1,0:T(8,128)}), f32[8,34,116]{2,1,0:T(8,128)S(1)}, u32[]{:S(2)}, u32[]{:S(2)}) %all-to-all-start.1) | async-done | bytes 126240 | tf_op jit(solution)/shard_map/all_to_all | solution.py:77
  29.8 0.7 gather_fusion.3
  30.8 1.3 %constant_dynamic-update-slice_fusion.6 = (f32[2,58,18,256]{3,1,2,0:T(8,128)S(1)}, f32[2,58,20,256]{3,1,2,0:T(8,128)S(1)}, f32[2,58,18,256]{3,1,2,0:T(8,128)S(1)}) fusion(f32[2,58,16,256]{3,2,1,0:T(8,128)S(1)} %copy-done, f32[2,58,20,256]{3,1,2,0:T(8,128)S(1)} %get-tuple-element.121, f32[2,58,18,256]{3,1,2,0:T(8,128)S(1)} %get-tuple-element.120), kind=kLoop, calls=%fused_computation.240 | loop fusion | bytes 8192000
  32.9 1.8 %fusion.44 = f32[2,58,18,256]{3,1,2,0:T(8,128)S(1)} fusion(f32[2,1,18,256]{3,1,2,0:T(1,128)S(1)} %get-tuple-element.78, f32[2,57,18,256]{3,1,2,0:T(8,128)S(1)} %get-tuple-element.80, f32[2,57,18,256]{3,1,2,0:T(8,128)S(1)} %get-tuple-element.79, f32[2,1,18,256]{3,1,2,0:T(1,128)S(1)} %get-tuple-element.77, f32[2,58,18,256]{3,1,2,0:T(8,128)S(1)} %get-tuple-element.115, ...), kind=kLoop, calls=%fused_computation.133 | loop fusion | flops 8017920 | bytes 13006848 | tf_op jit(solution)/shard_map/add | solution.py:49
  35.4 1.7 %fusion.80 = f32[2,58,16,256]{3,1,2,0:T(8,128)S(1)} fusion(f32[1,58,18,256]{3,1,2,0:T(8,128)S(1)} %get-tuple-element.88, f32[1,58,18,256]{3,1,2,0:T(8,128)S(1)} %get-tuple-element.87, f32[2,1,16,256]{3,1,2,0:T(1,128)S(1)} %get-tuple-element.96, f32[2,57,16,256]{3,1,2,0:T(8,128)S(1)} %fusion.60, f32[2,1,16,256]{3,1,2,0:T(1,128)S(1)} %get-tuple-element.95, ...), kind=kLoop, calls=%fused_computation.179 | loop fusion | flops 9027584 | bytes 6150144 | tf_op jit(solution)/shard_map/add | solution.py:49
  37.7 3.8 %collective-permute-start.3 = (f32[2,58,2,256]{3,1,2,0:T(8,128)S(1)}, f32[2,58,2,256]{3,1,2,0:T(8,128)S(1)}, u32[]{:S(2)}, u32[]{:S(2)}) collective-permute-start(f32[2,58,2,256]{3,1,2,0:T(8,128)S(1)} %get-tuple-element.111), channel_id=1, source_target_pairs={{1,0},{2,1},{3,2},{0,3},{5,4},{6,5},{7,6},{4,7},{9,8},{10,9},{11,1... | collective-permute-start | bytes 712712 | tf_op jit(solution)/shard_map/ppermute | solution.py:29
  41.5 7.2 %collective-permute-done.2 = f32[2,58,2,256]{3,1,2,0:T(8,128)S(1)} collective-permute-done((f32[2,58,2,256]{3,1,2,0:T(8,128)S(1)}, f32[2,58,2,256]{3,1,2,0:T(8,128)S(1)}, u32[]{:S(2)}, u32[]{:S(2)}) %collective-permute-start.2) | collective-permute-done | bytes 237600 | tf_op jit(solution)/shard_map/ppermute | solution.py:28
  48.7 2.6 %collective-permute-done.3 = f32[2,58,2,256]{3,1,2,0:T(8,128)S(1)} collective-permute-done((f32[2,58,2,256]{3,1,2,0:T(8,128)S(1)}, f32[2,58,2,256]{3,1,2,0:T(8,128)S(1)}, u32[]{:S(2)}, u32[]{:S(2)}) %collective-permute-start.3) | collective-permute-done | bytes 237600 | tf_op jit(solution)/shard_map/ppermute | solution.py:29
  51.6 0.6 fusion.109
  52.2 2.2 %fusion.10 = f32[2,58,18,256]{3,1,2,0:T(8,128)S(1)} fusion(f32[1,58,16,256]{3,1,2,0:T(8,128)S(1)} %get-tuple-element.104, f32[1,58,16,256]{3,1,2,0:T(8,128)S(1)} %get-tuple-element.103, f32[2,58,2,256]{3,1,2,0:T(8,128)S(1)} %collective-permute-done.2, f32[2,58,2,256]{3,1,2,0:T(8,128)S(1)} %collective-permute-done.3, ...), kind=kLoop, calls=%fused_computation.96 | loop fusion | flops 18708480 | bytes 11032576 | tf_op jit(solution)/shard_map/add | solution.py:49
  55.2 1.7 %fusion.75 = f32[2,58,16,256]{3,1,2,0:T(8,128)S(1)} fusion(f32[1,58,18,256]{3,1,2,0:T(8,128)S(1)} %get-tuple-element.86, f32[1,58,18,256]{3,1,2,0:T(8,128)S(1)} %get-tuple-element.85, f32[2,1,16,256]{3,1,2,0:T(1,128)S(1)} %get-tuple-element.94, f32[2,57,16,256]{3,1,2,0:T(8,128)S(1)} %fusion.56, f32[2,1,16,256]{3,1,2,0:T(1,128)S(1)} %get-tuple-element.93, ...), kind=kLoop, calls=%fused_computation.173 | loop fusion | flops 9027584 | bytes 6150144 | tf_op jit(solution)/shard_map/add | solution.py:49
  57.4 0.9 collective-permute-start.4
  58.3 3.0 %collective-permute-start.5 = (f32[2,58,2,256]{3,1,2,0:T(8,128)S(1)}, f32[2,58,2,256]{3,1,2,0:T(8,128)S(1)}, u32[]{:S(2)}, u32[]{:S(2)}) collective-permute-start(f32[2,58,2,256]{3,1,2,0:T(8,128)S(1)} %get-tuple-element.109), channel_id=1, source_target_pairs={{1,0},{2,1},{3,2},{0,3},{5,4},{6,5},{7,6},{4,7},{9,8},{10,9},{11,1... | collective-permute-start | bytes 712712 | tf_op jit(solution)/shard_map/ppermute | solution.py:29
  61.3 7.2 %collective-permute-done.4 = f32[2,58,2,256]{3,1,2,0:T(8,128)S(1)} collective-permute-done((f32[2,58,2,256]{3,1,2,0:T(8,128)S(1)}, f32[2,58,2,256]{3,1,2,0:T(8,128)S(1)}, u32[]{:S(2)}, u32[]{:S(2)}) %collective-permute-start.4) | collective-permute-done | bytes 237600 | tf_op jit(solution)/shard_map/ppermute | solution.py:28
  68.4 2.3 %collective-permute-done.5 = f32[2,58,2,256]{3,1,2,0:T(8,128)S(1)} collective-permute-done((f32[2,58,2,256]{3,1,2,0:T(8,128)S(1)}, f32[2,58,2,256]{3,1,2,0:T(8,128)S(1)}, u32[]{:S(2)}, u32[]{:S(2)}) %collective-permute-start.5) | collective-permute-done | bytes 237600 | tf_op jit(solution)/shard_map/ppermute | solution.py:29
  71.0 0.6 fusion.108
  71.6 2.2 %fusion.23 = f32[2,58,18,256]{3,1,2,0:T(8,128)S(1)} fusion(f32[1,58,16,256]{3,1,2,0:T(8,128)S(1)} %get-tuple-element.102, f32[1,58,16,256]{3,1,2,0:T(8,128)S(1)} %get-tuple-element.101, f32[2,58,2,256]{3,1,2,0:T(8,128)S(1)} %collective-permute-done.4, f32[2,58,2,256]{3,1,2,0:T(8,128)S(1)} %collective-permute-done.5, ...), kind=kLoop, calls=%fused_computation.109 | loop fusion | flops 18708480 | bytes 11032576 | tf_op jit(solution)/shard_map/add | solution.py:49
  74.6 1.7 %fusion.70 = f32[2,58,16,256]{3,1,2,0:T(8,128)S(1)} fusion(f32[1,58,18,256]{3,1,2,0:T(8,128)S(1)} %get-tuple-element.84, f32[1,58,18,256]{3,1,2,0:T(8,128)S(1)} %get-tuple-element.83, f32[2,1,16,256]{3,1,2,0:T(1,128)S(1)} %get-tuple-element.92, f32[2,57,16,256]{3,1,2,0:T(8,128)S(1)} %fusion.52, f32[2,1,16,256]{3,1,2,0:T(1,128)S(1)} %get-tuple-element.91, ...), kind=kLoop, calls=%fused_computation.167 | loop fusion | flops 9027584 | bytes 6150144 | tf_op jit(solution)/shard_map/add | solution.py:49
  76.7 1.7 %collective-permute-start.6 = (f32[2,58,2,256]{3,1,2,0:T(8,128)S(1)}, f32[2,58,2,256]{3,1,2,0:T(8,128)S(1)}, u32[]{:S(2)}, u32[]{:S(2)}) collective-permute-start(f32[2,58,2,256]{3,1,2,0:T(8,128)S(1)} %get-tuple-element.108), channel_id=1, source_target_pairs={{0,1},{1,2},{2,3},{3,0},{4,5},{5,6},{6,7},{7,4},{8,9},{9,10},{10,1... | collective-permute-start | bytes 712712 | tf_op jit(solution)/shard_map/ppermute | solution.py:28
  78.4 2.2 %collective-permute-start.7 = (f32[2,58,2,256]{3,1,2,0:T(8,128)S(1)}, f32[2,58,2,256]{3,1,2,0:T(8,128)S(1)}, u32[]{:S(2)}, u32[]{:S(2)}) collective-permute-start(f32[2,58,2,256]{3,1,2,0:T(8,128)S(1)} %get-tuple-element.107), channel_id=1, source_target_pairs={{1,0},{2,1},{3,2},{0,3},{5,4},{6,5},{7,6},{4,7},{9,8},{10,9},{11,1... | collective-permute-start | bytes 712712 | tf_op jit(solution)/shard_map/ppermute | solution.py:29
  80.6 1.9 %reduce_sum.47 = f32[2,58,256]{2,1,0:T(8,128)S(1)} reduce(f32[2,58,16,256]{3,2,1,0:T(8,128)} %param.11, f32[]{:T(128)} %constant.35.clone.1), dimensions={2}, to_apply=%region_8.9 | reduce | flops 445440 | bytes 2019332 | tf_op jit(solution)/shard_map/reduce_sum | solution.py:109
  82.4 5.3 %collective-permute-done.6 = f32[2,58,2,256]{3,1,2,0:T(8,128)S(1)} collective-permute-done((f32[2,58,2,256]{3,1,2,0:T(8,128)S(1)}, f32[2,58,2,256]{3,1,2,0:T(8,128)S(1)}, u32[]{:S(2)}, u32[]{:S(2)}) %collective-permute-start.6) | collective-permute-done | bytes 237600 | tf_op jit(solution)/shard_map/ppermute | solution.py:28
  87.8 3.6 %collective-permute-done.7 = f32[2,58,2,256]{3,1,2,0:T(8,128)S(1)} collective-permute-done((f32[2,58,2,256]{3,1,2,0:T(8,128)S(1)}, f32[2,58,2,256]{3,1,2,0:T(8,128)S(1)}, u32[]{:S(2)}, u32[]{:S(2)}) %collective-permute-start.7) | collective-permute-done | bytes 237600 | tf_op jit(solution)/shard_map/ppermute | solution.py:29
  91.5 0.6 fusion.107
  92.2 2.0 %fusion.36 = f32[2,58,18,256]{3,1,2,0:T(8,128)S(1)} fusion(f32[1,58,16,256]{3,1,2,0:T(8,128)S(1)} %get-tuple-element.100, f32[1,58,16,256]{3,1,2,0:T(8,128)S(1)} %get-tuple-element.99, f32[2,58,2,256]{3,1,2,0:T(8,128)S(1)} %collective-permute-done.6, f32[2,58,2,256]{3,1,2,0:T(8,128)S(1)} %collective-permute-done.7, ...), kind=kLoop, calls=%fused_computation.122 | loop fusion | flops 18708480 | bytes 11032576 | tf_op jit(solution)/shard_map/add | solution.py:49
  95.0 1.7 %fusion.65 = f32[2,58,16,256]{3,1,2,0:T(8,128)S(1)} fusion(f32[1,58,18,256]{3,1,2,0:T(8,128)S(1)} %get-tuple-element.82, f32[1,58,18,256]{3,1,2,0:T(8,128)S(1)} %get-tuple-element.81, f32[2,1,16,256]{3,1,2,0:T(1,128)S(1)} %get-tuple-element.90, f32[2,57,16,256]{3,1,2,0:T(8,128)S(1)} %fusion.48, f32[2,1,16,256]{3,1,2,0:T(1,128)S(1)} %get-tuple-element.89, ...), kind=kLoop, calls=%fused_computation.161 | loop fusion | flops 9027584 | bytes 6150144 | tf_op jit(solution)/shard_map/add | solution.py:49
  97.3 15.9 %all-gather = f32[8,58,256]{2,1,0:T(8,128)S(1)} all-gather(f32[2,58,256]{2,1,0:T(8,128)S(1)} %sub.260), channel_id=2, replica_groups=mesh['col'=8,'grp'=4] {'grp'}, dimensions={0}, use_global_device_ids=true | all-gather | bytes 593920 | tf_op jit(solution)/shard_map/all_gather | solution.py:16
  113.4 1.2 scatter_custom_fusion.1
  114.5 0.7 reshape.90
  115.2 3.4 %all-to-all-start.2 = ((f32[8,34,116]{2,1,0:T(8,128)}), f32[8,34,116]{2,1,0:T(8,128)S(1)}, u32[]{:S(2)}, u32[]{:S(2)}) async-start(f32[8,34,116]{2,1,0:T(8,128)} %reshape.90), calls=%async_computation.2 | async-start | bytes 327680 | tf_op jit(solution)/shard_map/all_to_all | solution.py:116
  118.6 2.4 %copy.78 = f32[2,58,16,256]{3,2,1,0:T(8,128)} copy(f32[2,58,16,256]{3,1,2,0:T(8,128)S(1)} %get-tuple-element.105) | data formatting | bytes 3801088
  121.0 3.4 %all-to-all-done.2 = f32[8,34,116]{2,1,0:T(8,128)S(1)} async-done(((f32[8,34,116]{2,1,0:T(8,128)}), f32[8,34,116]{2,1,0:T(8,128)S(1)}, u32[]{:S(2)}, u32[]{:S(2)}) %all-to-all-start.2) | async-done | bytes 126240 | tf_op jit(solution)/shard_map/all_to_all | solution.py:116
  124.4 0.7 gather_fusion.4
  125.1 0.8 copy.77
  (91 shorter events, 10.3 us)
Async XLA Ops:
  0.6 15.6 %copy-start.2 = (s32[2048]{0:T(1024)S(1)}, s32[2048]{0:T(1024)}, u32[]{:S(2)}) copy-start(s32[2048]{0:T(1024)} %param.9) | copy-start | bytes 24580
  0.6 11.4 %copy-start = (f32[2,58,16,256]{3,2,1,0:T(8,128)S(1)}, f32[2,58,16,256]{3,2,1,0:T(8,128)}, u32[]{:S(2)}) copy-start(f32[2,58,16,256]{3,2,1,0:T(8,128)} %param.11) | copy-start | bytes 5701636
  4.9 13.0 %copy-start.3 = (s32[256]{0:T(256)S(1)}, s32[256]{0:T(256)}, u32[]{:S(2)}) copy-start(s32[256]{0:T(256)} %param.10) | copy-start | bytes 3076
  4.9 13.0 %copy-start.1 = (f32[256,116]{0,1:T(8,128)S(1)}, f32[256,116]{0,1:T(8,128)}, u32[]{:S(2)}) copy-start(f32[256,116]{0,1:T(8,128)} %param.7) | copy-start | bytes 356356
  6.9 12.9 %all-to-all-start = ((f32[8,1,1972]{2,1,0:T(1,128)}), f32[8,1,1972]{2,1,0:T(1,128)S(1)}, u32[]{:S(2)}, u32[]{:S(2)}) async-start(f32[8,1,1972]{2,1,0:T(1,128)} %reshape.161), calls=%async_computation | async-start | bytes 131072 | tf_op jit(solution)/shard_map/all_to_all | solution.py:78
  12.3 18.4 %collective-permute-start = (f32[2,58,2,256]{3,1,2,0:T(8,128)S(1)}, f32[2,58,2,256]{3,1,2,0:T(8,128)S(1)}, u32[]{:S(2)}, u32[]{:S(2)}) collective-permute-start(f32[2,58,2,256]{3,1,2,0:T(8,128)S(1)} %copy.84), channel_id=1, source_target_pairs={{0,1},{1,2},{2,3},{3,0},{4,5},{5,6},{6,7},{7,4},{8,9},{9,10},{10,1... | collective-permute-start | bytes 712712 | tf_op jit(solution)/shard_map/ppermute | solution.py:28
  13.9 18.2 %collective-permute-start.1 = (f32[2,58,2,256]{3,1,2,0:T(8,128)S(1)}, f32[2,58,2,256]{3,1,2,0:T(8,128)S(1)}, u32[]{:S(2)}, u32[]{:S(2)}) collective-permute-start(f32[2,58,2,256]{3,1,2,0:T(8,128)S(1)} %copy.85), channel_id=1, source_target_pairs={{1,0},{2,1},{3,2},{0,3},{5,4},{6,5},{7,6},{4,7},{9,8},{10,9},{11,1... | collective-permute-start | bytes 712712 | tf_op jit(solution)/shard_map/ppermute | solution.py:29
  19.8 10.0 %all-to-all-start.1 = ((f32[8,34,116]{2,1,0:T(8,128)}), f32[8,34,116]{2,1,0:T(8,128)S(1)}, u32[]{:S(2)}, u32[]{:S(2)}) async-start(f32[8,34,116]{2,1,0:T(8,128)} %reshape.87), calls=%async_computation.1 | async-start | bytes 327680 | tf_op jit(solution)/shard_map/all_to_all | solution.py:77
  37.7 11.0 %collective-permute-start.2 = (f32[2,58,2,256]{3,1,2,0:T(8,128)S(1)}, f32[2,58,2,256]{3,1,2,0:T(8,128)S(1)}, u32[]{:S(2)}, u32[]{:S(2)}) collective-permute-start(f32[2,58,2,256]{3,1,2,0:T(8,128)S(1)} %get-tuple-element.112), channel_id=1, source_target_pairs={{0,1},{1,2},{2,3},{3,0},{4,5},{5,6},{6,7},{7,4},{8,9},{9,10},{10,1... | collective-permute-start | bytes 712712 | tf_op jit(solution)/shard_map/ppermute | solution.py:28
  37.7 13.6 %collective-permute-start.3 = (f32[2,58,2,256]{3,1,2,0:T(8,128)S(1)}, f32[2,58,2,256]{3,1,2,0:T(8,128)S(1)}, u32[]{:S(2)}, u32[]{:S(2)}) collective-permute-start(f32[2,58,2,256]{3,1,2,0:T(8,128)S(1)} %get-tuple-element.111), channel_id=1, source_target_pairs={{1,0},{2,1},{3,2},{0,3},{5,4},{6,5},{7,6},{4,7},{9,8},{10,9},{11,1... | collective-permute-start | bytes 712712 | tf_op jit(solution)/shard_map/ppermute | solution.py:29
  57.4 11.0 %collective-permute-start.4 = (f32[2,58,2,256]{3,1,2,0:T(8,128)S(1)}, f32[2,58,2,256]{3,1,2,0:T(8,128)S(1)}, u32[]{:S(2)}, u32[]{:S(2)}) collective-permute-start(f32[2,58,2,256]{3,1,2,0:T(8,128)S(1)} %get-tuple-element.110), channel_id=1, source_target_pairs={{0,1},{1,2},{2,3},{3,0},{4,5},{5,6},{6,7},{7,4},{8,9},{9,10},{10,1... | collective-permute-start | bytes 712712 | tf_op jit(solution)/shard_map/ppermute | solution.py:28
  58.3 12.4 %collective-permute-start.5 = (f32[2,58,2,256]{3,1,2,0:T(8,128)S(1)}, f32[2,58,2,256]{3,1,2,0:T(8,128)S(1)}, u32[]{:S(2)}, u32[]{:S(2)}) collective-permute-start(f32[2,58,2,256]{3,1,2,0:T(8,128)S(1)} %get-tuple-element.109), channel_id=1, source_target_pairs={{1,0},{2,1},{3,2},{0,3},{5,4},{6,5},{7,6},{4,7},{9,8},{10,9},{11,1... | collective-permute-start | bytes 712712 | tf_op jit(solution)/shard_map/ppermute | solution.py:29
  76.7 11.1 %collective-permute-start.6 = (f32[2,58,2,256]{3,1,2,0:T(8,128)S(1)}, f32[2,58,2,256]{3,1,2,0:T(8,128)S(1)}, u32[]{:S(2)}, u32[]{:S(2)}) collective-permute-start(f32[2,58,2,256]{3,1,2,0:T(8,128)S(1)} %get-tuple-element.108), channel_id=1, source_target_pairs={{0,1},{1,2},{2,3},{3,0},{4,5},{5,6},{6,7},{7,4},{8,9},{9,10},{10,1... | collective-permute-start | bytes 712712 | tf_op jit(solution)/shard_map/ppermute | solution.py:28
  78.4 13.0 %collective-permute-start.7 = (f32[2,58,2,256]{3,1,2,0:T(8,128)S(1)}, f32[2,58,2,256]{3,1,2,0:T(8,128)S(1)}, u32[]{:S(2)}, u32[]{:S(2)}) collective-permute-start(f32[2,58,2,256]{3,1,2,0:T(8,128)S(1)} %get-tuple-element.107), channel_id=1, source_target_pairs={{1,0},{2,1},{3,2},{0,3},{5,4},{6,5},{7,6},{4,7},{9,8},{10,9},{11,1... | collective-permute-start | bytes 712712 | tf_op jit(solution)/shard_map/ppermute | solution.py:29
  115.2 9.2 %all-to-all-start.2 = ((f32[8,34,116]{2,1,0:T(8,128)}), f32[8,34,116]{2,1,0:T(8,128)S(1)}, u32[]{:S(2)}, u32[]{:S(2)}) async-start(f32[8,34,116]{2,1,0:T(8,128)} %reshape.90), calls=%async_computation.2 | async-start | bytes 327680 | tf_op jit(solution)/shard_map/all_to_all | solution.py:116
